TPU v7x, 32 devices: a whole 2x2x4 slice. The times are simulated.
32 devices in a mesh: grp: 4 (over z), row: 8 (over y, x, core).
Axes of the slice: x: 2, y: 2, z: 4, core: 2. Of those that a mesh axis runs over, the one named last changes fastest.
Arguments:
- a_pieces: bfloat16 [4, 512, 4096], P('grp', 'row'), as said below
- touched: int32 [4, 512], P('grp', 'row'), may hold values from 0 to 7
- slot_row: int32 [512], P('row'), may hold values from 0 to 511, as said below
- x_blocks: bfloat16 [32, 64, 64], P('grp'), as said below
- z_inverse: bfloat16 [32, 64, 64], P('grp'), as said below
- block_class: int32 [32], P('grp'), may hold values from 0 to 1
Outputs:
- schur: float32 [512, 512], P('row', 'grp')
Inputs may be any that keep to these rules, and one draw needn't show every extreme that they name: `slot_row`: A permutation of the constraints. The 64 slots of one index r of row (slots r * 64 onward) hold, of the constraints o * 64 to (o + 1) * 64 - 1 of each index o, either none or exactly 16. `a_pieces`: each piece read as a 64 x 64 matrix is symmetric. `x_blocks`: each block is symmetric positive definite. `z_inverse`: each block is symmetric positive definite.
All inputs are finite; a program needn't handle non-finite values.
Results may differ from a plain program's by a relative error of at most 0.0008.
Values may be sent and summed in bfloat16 or wider, within the bound.
A program may use at most 64 MiB of HBM per device.

v0:
```python
import jax
import jax.numpy as jnp
from jax import lax
from jax.sharding import PartitionSpec as P


def masked_blocks(blocks, block_class):
    block_order = blocks.shape[1]
    positions = jnp.arange(block_order)
    active = block_order // 2 * (1 + block_class)
    inside = (positions[None, :, None] < active[:, None, None]) & (
        positions[None, None, :] < active[:, None, None]
    )
    return jnp.where(inside, blocks, jnp.zeros_like(blocks))


def shards(a_pieces, touched, slot_row, x_blocks, z_inverse, block_class):
    local_rows = a_pieces.shape[1]
    block_order = x_blocks.shape[1]
    flat_len = a_pieces.shape[2]
    x_masked = masked_blocks(x_blocks, block_class)
    z_masked = masked_blocks(z_inverse, block_class)
    own_block = touched[0]
    a_local = a_pieces[0]
    pieces = a_local.reshape(local_rows, block_order, block_order)
    left_part = jnp.einsum(
        "rab,rbc->rac", x_masked[own_block], pieces, preferred_element_type=jnp.float32
    ).astype(jnp.bfloat16)
    product = jnp.einsum(
        "rab,rbc->rac", left_part, z_masked[own_block], preferred_element_type=jnp.float32
    ).astype(jnp.bfloat16)
    product_flat = product.reshape(local_rows, flat_len)
    all_slots, all_kinds = (
        lax.all_gather(slot_row, "row", axis=0, tiled=True),
        lax.all_gather(touched, "row", axis=1, tiled=True),
    )
    constraints = all_slots.shape[0]
    kinds_flat = all_kinds[0]
    scores = lax.dot_general(
        product_flat,
        lax.all_gather(a_local, "row", axis=0, tiled=True),
        (((1,), (1,)), ((), ())),
        preferred_element_type=jnp.float32,
    )
    scores = jnp.where(own_block[:, None] == kinds_flat[None, :], scores, jnp.zeros_like(scores))
    inverse = (
        jnp.zeros((constraints,), jnp.int32)
        .at[all_slots]
        .set(jnp.arange(constraints, dtype=jnp.int32))
    )
    ordered = scores[:, inverse]
    summed = lax.psum_scatter(ordered, "grp", scatter_dimension=1, tiled=True)
    columns = summed.shape[1]
    devices = lax.axis_size("row")
    slot_cap = max(2, local_rows // devices * 2)
    owners = slot_row // local_rows
    earlier = jnp.arange(local_rows)[None, :] < jnp.arange(local_rows)[:, None]
    rank_send = jnp.sum(((owners[:, None] == owners[None, :]) & earlier).astype(jnp.int32), axis=1)
    send_slot = owners * slot_cap + rank_send
    outgoing = jnp.zeros((devices * slot_cap, columns), jnp.float32).at[send_slot].set(summed)
    incoming = lax.all_to_all(outgoing, "row", split_axis=0, concat_axis=0, tiled=True)
    my_row = lax.axis_index("row")
    table_ids = all_slots.reshape(devices, local_rows)
    arrives = table_ids // local_rows == my_row
    rank_recv = jnp.cumsum(arrives.astype(jnp.int32), axis=1) - 1
    source_base = (jnp.arange(devices, dtype=jnp.int32) * slot_cap)[:, None]
    target = jnp.where(arrives, source_base + rank_recv, devices * slot_cap)
    landing = jnp.full((devices * slot_cap + 1,), local_rows, jnp.int32)
    landing = landing.at[target.reshape(-1)].set((table_ids % local_rows).reshape(-1))
    result = (
        jnp.zeros((local_rows, columns), jnp.float32).at[landing[:-1]].set(incoming, mode="drop")
    )
    return result


def solution(mesh):
    return jax.shard_map(
        shards,
        mesh=mesh,
        in_specs=(
            P("grp", "row", None),
            P("grp", "row"),
            P("row"),
            P("grp", None, None),
            P("grp", None, None),
            P("grp"),
        ),
        out_specs=P("row", "grp"),
        check_vma=False,
    )
```

profile of v0, /device:TPU:0, one launch (start us, length us, event | category | flops | bytes accessed | tf_op | source)
XLA Modules:
  0.0 93.4 jit_solution(4507066098227181438)
XLA Ops:
  6.5 0.7 all-gather.3.cloned.1.call-update
  7.3 0.0 reduce-scatter.2.cloned.1.call-start
  7.3 2.1 %reshape_squeeze.3 = bf16[64,64,64]{2,1,0:T(8,128)(2,1)S(1)} reshape(bf16[1,64,4096]{2,1,0:T(8,128)(2,1)} %param.6) | data formatting | bytes 1048576 | tf_op jit(solution)/shard_map/reshape;squeeze | solution.py:25
  9.4 1.2 %dynamic-slice = u32[1]{0:T(128)} dynamic-slice(u32[32]{0:T(128)} %constant.77, u32[]{:T(128)S(6)} %add.84), dynamic_slice_sizes={1} | dynamic-slice | bytes 12
  11.3 0.9 dynamic-update-slice
  12.1 0.7 bitcast_dynamic-update-slice_fusion
  12.9 9.5 %all-reduce.2 = (s32[512]{0:T(512)S(1)}, s32[512]{0:T(512)S(1)}) all-reduce(s32[512]{0:T(512)S(1)} %dynamic-update-slice, s32[512]{0:T(512)S(1)} %bitcast_dynamic-update-slice_fusion), channel_id=1, replica_groups=mesh['grp'=4,'row'=8] {'row'}, use_global_device_ids=true, to_apply=%add | all-reduce | flops 1024 | bytes 8192
  22.4 0.1 reshape.95
  22.5 0.2 reduce_window_sum.11
  22.7 0.1 add_add_fusion
  22.8 0.1 add.71
  22.8 0.7 fusion.18
  23.5 0.7 add_multiply_fusion
  24.2 0.1 iota_compare_fusion.1
  24.2 1.1 %and_select_fusion.1 = (bf16[8,64,64]{2,1,0:T(8,128)(2,1)S(1)}, bf16[8,64,64]{2,1,0:T(8,128)(2,1)S(1)}) fusion(bf16[8,64,64]{2,1,0:T(8,128)(2,1)} %param.9, pred[8,64]{1,0:T(8,128)(4,1)S(1)} %iota_compare_fusion.1, bf16[8,64,64]{2,1,0:T(8,128)(2,1)} %param.10), kind=kLoop, calls=%fused_computation.13 | loop fusion | flops 98304 | bytes 262656 | tf_op jit(solution)/shard_map/jit(_where)/select_n | solution.py:14
  25.4 0.7 gather_fusion.1
  26.1 0.7 gather_fusion
  26.9 1.7 %convolution_convert_fusion = bf16[64,64,64]{2,1,0:T(8,128)(2,1)} fusion(bf16[64,64,64]{2,1,0:T(8,128)(2,1)S(1)} %gather_fusion.1, bf16[64,64,64]{2,1,0:T(8,128)(2,1)S(1)} %gather_fusion, bf16[64,64,64]{2,1,0:T(8,128)(2,1)S(1)} %reshape_squeeze.3), kind=kOutput, calls=%fused_computation.9 | convolution fusion | flops 67633152 | bytes 2097152 | tf_op jit(solution)/shard_map/rab,rbc->rac/dot_general | solution.py:29
  28.6 2.1 %reshape.96 = bf16[64,4096]{1,0:T(8,128)(2,1)S(1)} reshape(bf16[64,64,64]{2,1,0:T(8,128)(2,1)} %convolution_convert_fusion) | data formatting | bytes 1048576 | tf_op jit(solution)/shard_map/reshape | solution.py:32
  30.7 2.4 %scatter_custom_fusion.1 = s32[512]{0:T(512)S(1)} fusion(s32[512]{0:T(512)S(1)} %get-tuple-element.7, s32[512]{0:T(512)S(1)} %iota.33, s32[]{:T(128)} %constant.35.clone.1), kind=kCustom, calls=%fused_computation.52 | custom fusion | bytes 2052 | tf_op jit(solution)/shard_map/scatter | solution.py:49
  33.2 15.4 %all-gather.3.cloned.1.call-done = bf16[1,512,4096]{2,1,0:T(8,128)(2,1)} async-done(((bf16[1,64,4096]{2,1,0:T(8,128)(2,1)}), bf16[1,512,4096]{2,1,0:T(8,128)(2,1)}) %all-gather.3.cloned.1.call-update) | async-done | bytes 4194320 | tf_op jit(solution)/shard_map/all_gather | solution.py:41
  48.6 3.6 %fusion.2 = f32[64,512]{1,0:T(8,128)S(1)} fusion(bf16[64,4096]{1,0:T(8,128)(2,1)S(1)} %reshape.96, bf16[1,512,4096]{2,1,0:T(8,128)(2,1)} %all-gather.3.cloned.1.call-done, s32[512]{0:T(512)S(1)} %get-tuple-element.6, s32[64]{0:T(128)S(1)} %bitcast.21), kind=kOutput, calls=%fused_computation.11 | convolution fusion | flops 268500992 | bytes 4851968 | tf_op jit(solution)/shard_map/dot_general | solution.py:39
  52.2 0.1 copy.10
  52.3 1.6 %gather_fusion.2 = f32[512,64]{1,0:T(8,128)} fusion(f32[64,512]{0,1:T(8,128)S(1)} %copy.10, s32[1024]{0:T(1024)S(1)} %pad_clamp_fusion), kind=kCustom, calls=%fused_computation.2 | custom fusion | bytes 264192 | tf_op jit(solution)/shard_map/gather | solution.py:51
  54.0 0.2 convert_reduce_fusion
  54.2 2.4 %scatter_custom_fusion = s32[129]{0:T(256)S(1)} fusion(s32[512]{0:T(512)S(1)} %get-tuple-element.9, s32[512]{0:T(512)S(1)} %get-tuple-element.8, s32[]{:T(128)} %constant.33.clone.1), kind=kCustom, calls=%fused_computation.58 | custom fusion | bytes 520 | tf_op jit(solution)/shard_map/scatter | solution.py:69
  56.6 17.5 %reduce-scatter.2.cloned.1.call-done = f32[64,128]{0,1:T(8,128)} async-done(((f32[64,512]{0,1:T(8,128)}), f32[64,128]{0,1:T(8,128)}) %reduce-scatter.2.cloned.1.call-update) | async-done | bytes 32784 | tf_op jit(solution)/shard_map/reduce_scatter | solution.py:52
  74.1 0.9 copy.11
  75.0 1.3 %scatter_custom_fusion.2 = f32[128,128]{1,0:T(8,128)} fusion(s32[64]{0:T(128)S(1)} %compare_select_fusion.3, f32[64,128]{1,0:T(8,128)S(1)} %copy.11, f32[]{:T(128)} %constant.31.clone.1), kind=kCustom, calls=%fused_computation.16 | custom fusion | bytes 65540 | tf_op jit(solution)/shard_map/scatter | solution.py:60
  76.4 3.7 %all-to-all-start = ((f32[8,16,128]{2,1,0:T(8,128)}), f32[8,16,128]{2,1,0:T(8,128)S(1)}, u32[]{:S(2)}, u32[]{:S(2)}) async-start(f32[8,16,128]{2,1,0:T(8,128)} %bitcast.6), calls=%async_computation.1 | async-start | bytes 131072 | tf_op jit(solution)/shard_map/all_to_all | solution.py:61
  80.1 5.0 %all-to-all-done = f32[8,16,128]{2,1,0:T(8,128)S(1)} async-done(((f32[8,16,128]{2,1,0:T(8,128)}), f32[8,16,128]{2,1,0:T(8,128)S(1)}, u32[]{:S(2)}, u32[]{:S(2)}) %all-to-all-start) | async-done | bytes 65568 | tf_op jit(solution)/shard_map/all_to_all | solution.py:61
  85.1 1.4 %scatter_custom_fusion.3 = f32[64,128]{1,0:T(8,128)} fusion(s32[128]{0:T(128)S(1)} %compare_select_fusion.4, f32[128,128]{1,0:T(8,128)S(1)} %bitcast.20, f32[]{:T(128)} %constant.31.clone.1), kind=kCustom, calls=%fused_computation.19 | custom fusion | bytes 32772 | tf_op jit(solution)/shard_map/scatter | solution.py:71
  (18 shorter events, 0.1 us)
Async XLA Ops:
  6.5 42.1 %all-gather.3.cloned.1.call-start = ((), (), s32[]{:S(2)}) async-start(), calls=%async_computation.3 | async-start | bytes 4718592 | tf_op jit(solution)/shard_map/all_gather | solution.py:41
  7.3 66.9 %reduce-scatter.2.cloned.1.call-start = ((), (), s32[]{:S(2)}) async-start(), calls=%async_computation.2 | async-start | bytes 327680 | tf_op jit(solution)/shard_map/reduce_scatter | solution.py:52
  26.1 7.0 %copy-start.1 = (s32[64]{0:T(128)S(1)}, s32[64]{0:T(128)}, u32[]{:S(2)}) copy-start(s32[64]{0:T(128)} %param.8) | copy-start | bytes 772
  26.1 22.5 %copy-start = (s32[1,64]{1,0:T(1,128)S(1)}, s32[1,64]{1,0:T(1,128)}, u32[]{:S(2)}) copy-start(s32[1,64]{1,0:T(1,128)} %param.7) | copy-start | bytes 772
  76.4 8.7 %all-to-all-start = ((f32[8,16,128]{2,1,0:T(8,128)}), f32[8,16,128]{2,1,0:T(8,128)S(1)}, u32[]{:S(2)}, u32[]{:S(2)}) async-start(f32[8,16,128]{2,1,0:T(8,128)} %bitcast.6), calls=%async_computation.1 | async-start | bytes 131072 | tf_op jit(solution)/shard_map/all_to_all | solution.py:61
Sparse Core Ops, SparseCore 0:
  9.2 39.3 all-gather.2
  54.1 19.9 reduce-scatter.1
where the time goes:
time: 93.7 us; the launch traced here: 93.4 us
  waiting for transfers between devices  38.7 us (41%)
  local copies, waits for them, and re-layouts  19 us (20%)
  between operations  14.2 us (15%)
  blocking collectives  9.49 us (10%)
  matrix products  5.27 us (6%)
  starting transfers between devices  3.72 us (4%)
  other arithmetic  3.04 us (3%)
    reduce_scatter x1, waiting for transfers between devices, shards(): summed = lax.psum_scatter(ordered, 'grp', scatter_dimension=1, tiled=True)  17.5 us
    all_gather x1, waiting for transfers between devices, shards(): lax.all_gather(a_local, 'row', axis=0, tiled=True)  15.4 us
    unnamed x1, blocking collectives  9.49 us
    all_to_all x1, waiting for transfers between devices, shards(): lax.all_to_all(outgoing, 'row', split_axis=0, concat_axis=0, tiled=True)  5.01 us
    all_to_all x1, starting transfers between devices, shards(): lax.all_to_all(outgoing, 'row', split_axis=0, concat_axis=0, tiled=True)  3.68 us
    dot_general x1, matrix products, shards(): lax.dot_general(product_flat, lax.all_gather(a_local, 'row', axis=0, tile...  3.58 us
    unnamed x9, local copies, waits for them, and re-layouts  2.86 us
    scatter x1, local copies, waits for them, and re-layouts, shards(): landing.at[target.reshape(-1)].set((table_ids % local_rows).reshape(-1))  2.44 us
  transfers between devices with their start and end apart: 3, of which 3 were waited for; matrix products, arithmetic and copies ran while one was open for 20% of the time, Pallas kernels for 0%

commit v1 on v0

--- a/solution.py
+++ b/solution.py
@@ -2,6 +2,12 @@
 import jax.numpy as jnp
 from jax import lax
 from jax.sharding import PartitionSpec as P
+
+
+def mark_clusters(v0):
+    return jnp.concatenate(
+        jax.lax.all_to_all(jnp.stack(jax.lax.axis_size("row") * [v0]), "row", 0, 0), axis=0
+    )
 
 
 def masked_blocks(blocks, block_class):
@@ -38,7 +44,7 @@
     kinds_flat = all_kinds[0]
     scores = lax.dot_general(
         product_flat,
-        lax.all_gather(a_local, "row", axis=0, tiled=True),
+        mark_clusters(a_local),
         (((1,), (1,)), ((), ())),
         preferred_element_type=jnp.float32,
     )

time: 93.7 us -> 121 us (1.29)
  blocking collectives: 9.49 us -> 48.5 us
  waiting for transfers between devices: 38.7 us -> 22.7 us
  starting transfers between devices: 3.72 us -> 9.03 us
  other arithmetic: 3.04 us -> 1.43 us
    unnamed x1, blocking collectives: 9.49 us -> 48.5 us
    all_gather x1 -> x0, waiting for transfers between devices: 15.4 us -> none  [shards(): lax.all_gather(a_local, 'row', axis=0, tiled=True)]
    all_to_all x0 -> x1, starting transfers between devices: none -> 5.34 us  [mark_clusters(): jax.lax.all_to_all(jnp.stack(jax.lax.axis_size('row') * [v0]), 'row', 0, 0)]
    another operation x0 -> x1, local copies, waits for them, and re-layouts: none -> 3.54 us  [mark_clusters(): jnp.stack(jax.lax.axis_size('row') * [v0])]
    unnamed x9 -> x21, local copies, waits for them, and re-layouts: 2.86 us -> 0.95 us
  transfers between devices with their start and end apart: 3 -> 3, of which waited for: 3 -> 2; matrix products, arithmetic and copies ran while one was open for 20% -> 11% of each run, Pallas kernels for 0% -> 0%
where the time goes in v1:
time: 121 us
  blocking collectives  48.5 us (40%)
  waiting for transfers between devices  22.7 us (19%)
  local copies, waits for them, and re-layouts  19.7 us (16%)
  between operations  14.3 us (12%)
  starting transfers between devices  9.03 us (7%)
  matrix products  5.39 us (4%)
  other arithmetic  1.43 us (1%)
    unnamed x1, blocking collectives  48.5 us
    reduce_scatter x1, waiting for transfers between devices, shards(): summed = lax.psum_scatter(ordered, 'grp', scatter_dimension=1, tiled=True)  17.7 us
    all_to_all x1, starting transfers between devices, mark_clusters(): jax.lax.all_to_all(jnp.stack(jax.lax.axis_size('row') * [v0]), 'row', 0, 0)  5.34 us
    all_to_all x1, waiting for transfers between devices, shards(): lax.all_to_all(outgoing, 'row', split_axis=0, concat_axis=0, tiled=True)  5.01 us
    all_to_all x1, starting transfers between devices, shards(): lax.all_to_all(outgoing, 'row', split_axis=0, concat_axis=0, tiled=True)  3.65 us
    dot_general x1, matrix products, shards(): lax.dot_general(product_flat, mark_clusters(a_local), (((1,), (1,)), ((),...  3.59 us
    another operation x1, local copies, waits for them, and re-layouts, mark_clusters(): jnp.stack(jax.lax.axis_size('row') * [v0])  3.54 us
    scatter x1, local copies, waits for them, and re-layouts, shards(): landing.at[target.reshape(-1)].set((table_ids % local_rows).reshape(-1))  2.44 us
  transfers between devices with their start and end apart: 3, of which 2 were waited for; matrix products, arithmetic and copies ran while one was open for 11% of the time, Pallas kernels for 0%

profile of v1, /device:TPU:0, one launch (start us, length us, event | category | flops | bytes accessed | tf_op | source)
XLA Modules:
  0.0 121.0 jit_solution(15557534788435186210)
XLA Ops:
  6.5 3.5 %stack.3 = bf16[8,64,4096]{2,1,0:T(8,128)(2,1)} broadcast(bf16[64,4096]{1,0:T(8,128)(2,1)} %bitcast.17), dimensions={1,2} | broadcast | bytes 4718592 | tf_op jit(solution)/shard_map/stack | solution.py:9
  10.1 5.3 %all-to-all-start = ((bf16[8,64,4096]{2,1,0:T(8,128)(2,1)}), bf16[8,64,4096]{2,1,0:T(8,128)(2,1)}, u32[]{:S(2)}, u32[]{:S(2)}) async-start(bf16[8,64,4096]{2,1,0:T(8,128)(2,1)} %stack.3), calls=%async_computation | async-start | bytes 8388608 | tf_op jit(solution)/shard_map/all_to_all | solution.py:9
  15.5 0.0 reduce-scatter.2.cloned.1.call-start
  15.5 1.1 reshape_squeeze.3
  16.7 0.6 dynamic-slice
  17.9 0.2 dynamic-update-slice
  18.2 0.1 bitcast_dynamic-update-slice_fusion
  18.3 48.5 %all-reduce.2 = (s32[512]{0:T(512)S(1)}, s32[512]{0:T(512)S(1)}) all-reduce(s32[512]{0:T(512)S(1)} %dynamic-update-slice, s32[512]{0:T(512)S(1)} %bitcast_dynamic-update-slice_fusion), channel_id=1, replica_groups=mesh['grp'=4,'row'=8] {'row'}, use_global_device_ids=true, to_apply=%add | all-reduce | flops 1024 | bytes 8192
  66.8 0.1 reshape.99
  66.9 0.2 reduce_window_sum.11
  67.1 0.1 add_add_fusion
  67.2 0.1 add.71
  67.3 0.1 iota_compare_fusion.1
  67.4 0.1 and_select_fusion.1
  67.5 0.7 gather_fusion.1
  68.3 0.7 gather_fusion
  69.0 1.8 %convolution_convert_fusion = bf16[64,64,64]{2,1,0:T(8,128)(2,1)} fusion(bf16[64,64,64]{2,1,0:T(8,128)(2,1)S(1)} %gather_fusion.1, bf16[64,64,64]{2,1,0:T(8,128)(2,1)S(1)} %gather_fusion, bf16[64,64,64]{2,1,0:T(8,128)(2,1)S(1)} %reshape_squeeze.3), kind=kOutput, calls=%fused_computation.7 | convolution fusion | flops 67633152 | bytes 2097152 | tf_op jit(solution)/shard_map/rab,rbc->rac/dot_general | solution.py:35
  70.9 2.1 %reshape.100 = bf16[64,4096]{1,0:T(8,128)(2,1)S(1)} reshape(bf16[64,64,64]{2,1,0:T(8,128)(2,1)} %convolution_convert_fusion) | data formatting | bytes 1048576 | tf_op jit(solution)/shard_map/reshape | solution.py:38
  73.0 2.4 %scatter_custom_fusion.1 = s32[512]{0:T(512)S(1)} fusion(s32[512]{0:T(512)S(1)} %get-tuple-element.7, s32[512]{0:T(512)S(1)} %iota.33, s32[]{:T(128)} %constant.35.clone.1), kind=kCustom, calls=%fused_computation.50 | custom fusion | bytes 2052 | tf_op jit(solution)/shard_map/scatter | solution.py:55
  75.4 0.7 and_select_fusion.2
  76.1 3.6 %convolution_select_fusion = f32[64,512]{1,0:T(8,128)S(1)} fusion(bf16[64,4096]{1,0:T(8,128)(2,1)S(1)} %reshape.100, bf16[512,4096]{1,0:T(8,128)(2,1)} %bitcast.5, s32[512]{0:T(512)S(1)} %get-tuple-element.6, s32[64]{0:T(128)} %bitcast.20), kind=kOutput, calls=%fused_computation.9 | convolution fusion | flops 268500992 | bytes 4851968 | tf_op jit(solution)/shard_map/dot_general | solution.py:45
  79.7 0.1 copy.10
  79.8 1.6 %gather_fusion.2 = f32[512,64]{1,0:T(8,128)} fusion(f32[64,512]{0,1:T(8,128)S(1)} %copy.10, s32[1024]{0:T(1024)S(1)} %pad_clamp_fusion), kind=kCustom, calls=%fused_computation.2 | custom fusion | bytes 264192 | tf_op jit(solution)/shard_map/gather | solution.py:57
  81.5 0.0 reduce-scatter.2.cloned.1.call-update
  81.5 0.2 convert_reduce_fusion
  81.7 2.4 %scatter_custom_fusion = s32[129]{0:T(256)S(1)} fusion(s32[512]{0:T(512)S(1)} %get-tuple-element.9, s32[512]{0:T(512)S(1)} %get-tuple-element.8, s32[]{:T(128)} %constant.33.clone.1), kind=kCustom, calls=%fused_computation.56 | custom fusion | bytes 520 | tf_op jit(solution)/shard_map/scatter | solution.py:75
  84.1 17.7 %reduce-scatter.2.cloned.1.call-done = f32[64,128]{0,1:T(8,128)} async-done(((f32[64,512]{0,1:T(8,128)}), f32[64,128]{0,1:T(8,128)}) %reduce-scatter.2.cloned.1.call-update) | async-done | bytes 32784 | tf_op jit(solution)/shard_map/reduce_scatter | solution.py:58
  101.9 0.9 copy.11
  102.8 1.3 %scatter_custom_fusion.2 = f32[128,128]{1,0:T(8,128)} fusion(s32[64]{0:T(128)S(1)} %compare_select_fusion.3, f32[64,128]{1,0:T(8,128)S(1)} %copy.11, f32[]{:T(128)} %constant.31.clone.1), kind=kCustom, calls=%fused_computation.14 | custom fusion | bytes 65540 | tf_op jit(solution)/shard_map/scatter | solution.py:66
  104.1 3.6 %all-to-all-start.1 = ((f32[8,16,128]{2,1,0:T(8,128)}), f32[8,16,128]{2,1,0:T(8,128)S(1)}, u32[]{:S(2)}, u32[]{:S(2)}) async-start(f32[8,16,128]{2,1,0:T(8,128)} %bitcast.7), calls=%async_computation.2 | async-start | bytes 131072 | tf_op jit(solution)/shard_map/all_to_all | solution.py:67
  107.7 5.0 %all-to-all-done.1 = f32[8,16,128]{2,1,0:T(8,128)S(1)} async-done(((f32[8,16,128]{2,1,0:T(8,128)}), f32[8,16,128]{2,1,0:T(8,128)S(1)}, u32[]{:S(2)}, u32[]{:S(2)}) %all-to-all-start.1) | async-done | bytes 65568 | tf_op jit(solution)/shard_map/all_to_all | solution.py:67
  112.8 1.4 %scatter_custom_fusion.3 = f32[64,128]{1,0:T(8,128)} fusion(s32[128]{0:T(128)S(1)} %compare_select_fusion.4, f32[128,128]{1,0:T(8,128)S(1)} %bitcast.19, f32[]{:T(128)} %constant.31.clone.1), kind=kCustom, calls=%fused_computation.17 | custom fusion | bytes 32772 | tf_op jit(solution)/shard_map/scatter | solution.py:77
  (30 shorter events, 0.1 us)
Async XLA Ops:
  10.1 5.4 %copy-start = (bf16[1,64,4096]{2,1,0:T(8,128)(2,1)S(1)}, bf16[1,64,4096]{2,1,0:T(8,128)(2,1)}, u32[]{:S(2)}) copy-start(bf16[1,64,4096]{2,1,0:T(8,128)(2,1)} %param.6) | copy-start | bytes 1572868
  10.1 6.6 %copy-start.7 = (u32[32]{0:T(128)S(1)}, u32[32]{0:T(128)}, u32[]{:S(2)}) copy-start(u32[32]{0:T(128)} %constant.77) | copy-start | bytes 388
  10.1 7.8 %copy-start.5 = (s32[64]{0:T(128)S(1)}, s32[64]{0:T(128)}, u32[]{:S(2)}) copy-start(s32[64]{0:T(128)} %param.8) | copy-start | bytes 772
  10.1 8.1 %copy-start.3 = (s32[1,64]{1,0:T(1,128)S(1)}, s32[1,64]{1,0:T(1,128)}, u32[]{:S(2)}) copy-start(s32[1,64]{1,0:T(1,128)} %param.7) | copy-start | bytes 772
  10.1 57.2 %copy-start.4 = (s32[8]{0:T(128)S(1)}, s32[8]{0:T(128)}, u32[]{:S(2)}) copy-start(s32[8]{0:T(128)} %param.11) | copy-start | bytes 100
  10.1 57.3 %copy-start.1 = (bf16[8,64,64]{2,1,0:T(8,128)(2,1)S(1)}, bf16[8,64,64]{2,1,0:T(8,128)(2,1)}, u32[]{:S(2)}) copy-start(bf16[8,64,64]{2,1,0:T(8,128)(2,1)} %param.9) | copy-start | bytes 196612
  10.1 57.3 %copy-start.2 = (bf16[8,64,64]{2,1,0:T(8,128)(2,1)S(1)}, bf16[8,64,64]{2,1,0:T(8,128)(2,1)}, u32[]{:S(2)}) copy-start(bf16[8,64,64]{2,1,0:T(8,128)(2,1)} %param.10) | copy-start | bytes 196612
  10.1 66.0 %all-to-all-start = ((bf16[8,64,4096]{2,1,0:T(8,128)(2,1)}), bf16[8,64,4096]{2,1,0:T(8,128)(2,1)}, u32[]{:S(2)}, u32[]{:S(2)}) async-start(bf16[8,64,4096]{2,1,0:T(8,128)(2,1)} %stack.3), calls=%async_computation | async-start | bytes 8388608 | tf_op jit(solution)/shard_map/all_to_all | solution.py:9
  15.5 86.4 %reduce-scatter.2.cloned.1.call-start = ((), (), s32[]{:S(2)}) async-start(), calls=%async_computation.3 | async-start | bytes 327680 | tf_op jit(solution)/shard_map/reduce_scatter | solution.py:58
  70.8 13.3 %copy-start.6 = (s32[64]{0:T(128)S(1)}, s32[64]{0:T(128)}, u32[]{:S(2)}) copy-start(s32[64]{0:T(128)} %param.8) | copy-start | bytes 772
  104.1 8.7 %all-to-all-start.1 = ((f32[8,16,128]{2,1,0:T(8,128)}), f32[8,16,128]{2,1,0:T(8,128)S(1)}, u32[]{:S(2)}, u32[]{:S(2)}) async-start(f32[8,16,128]{2,1,0:T(8,128)} %bitcast.7), calls=%async_computation.2 | async-start | bytes 131072 | tf_op jit(solution)/shard_map/all_to_all | solution.py:67
Sparse Core Ops, SparseCore 0:
  81.6 20.1 reduce-scatter.1
